TPU v7x, 32 devices: a whole 2x2x4 slice. The times are simulated.
32 devices in a mesh: rows: 4 (over x, core), cols: 8 (over z, y).
Axes of the slice: x: 2, y: 2, z: 4, core: 2. Of those that a mesh axis runs over, the one named last changes fastest.
Arguments:
- samples: bfloat16 [2048, 65536], P('rows', 'cols'), may hold values from -0.0234375 to 0.0234375
- labels: int32 [2048], P('rows'), may hold values 0 or 1
- weights: float32 [65536], P('cols'), may hold values from -7 to 7, as said below
- hist_s: float32 [16, 65536], P(None, 'cols'), may hold values from -60 to 60
- hist_y: float32 [16, 65536], P(None, 'cols'), may hold values from -480 to 480, as said below
- counter: int32 [1], replicated, may hold values from 0 to 4095
Outputs:
- new_weights: float32 [65536], P('cols')
- gradient: float32 [65536], P('cols')
Inputs may be any that keep to these rules, and one draw needn't show every extreme that they name: weights share a common direction with the rows of hist_s. Each entry of hist_y[j] is a positive multiple of the same entry of hist_s[j], so s_j . y_j > 0.
All inputs are finite; a program needn't handle non-finite values. No bound on the sum of `labels` on one device may be relied on, other than what follows from the above.
Results may differ from a plain program's by a relative error of at most 0.0013.
Values sent between devices are 32-bit elements; how exact they have to be, the bound alone decides.
A program may use at most 64 MiB of HBM per device.

v0:
```python
import jax
import jax.numpy as jnp
from jax import lax
from jax.sharding import PartitionSpec as P

HIST = 16
penalty = 4.0
step_length = 0.5
highest = lax.Precision.HIGHEST


def row_share(values):
    width = values.shape[-1] // lax.axis_size("rows")
    return lax.dynamic_slice_in_dim(values, lax.axis_index("rows") * width, width, values.ndim - 1)


def quad_form(left, matrix, right):
    return jnp.dot(left, jnp.dot(matrix, right, precision=highest), precision=highest)


def gram_recursion(gram, basis, newest):
    count = 2 * HIST + 1
    places = jnp.arange(count, dtype=jnp.int32)
    select_s = (places == newest).astype(jnp.float32)
    select_y = (places == newest + HIST).astype(jnp.float32)
    gamma = quad_form(select_s, gram, select_y) / quad_form(select_y, gram, select_y)
    weights_of = (places == 2 * HIST).astype(jnp.float32)
    coefs = []
    pairs = []
    for step in range(HIST):
        slot = (newest - step) % HIST
        pick_s = (places == slot).astype(jnp.float32)
        pick_y = (places == slot + HIST).astype(jnp.float32)
        rho = 1.0 / quad_form(pick_s, gram, pick_y)
        coef = rho * quad_form(pick_s, gram, weights_of)
        coefs.append(coef)
        pairs.append((pick_s, pick_y, rho))
        weights_of = weights_of - coef * pick_y
    result_of = gamma * weights_of
    for step in reversed(range(HIST)):
        pick_s, pick_y, rho = pairs[step]
        beta = rho * quad_form(pick_y, gram, result_of)
        result_of = result_of + (coefs[step] - beta) * pick_s
    return jnp.dot(result_of, basis, precision=highest)


def body(samples, labels, weights, hist_s, hist_y, counter):
    margin_part = jnp.dot(samples, weights.astype(jnp.bfloat16), preferred_element_type=jnp.float32)
    margin = lax.psum(margin_part, "cols")
    resid = (jax.nn.sigmoid(margin) - labels.astype(jnp.float32)).astype(jnp.bfloat16)
    total_part = jnp.dot(resid, samples, preferred_element_type=jnp.float32)
    newest = counter[0] % HIST
    total = lax.psum(total_part, "rows")
    gradient = weights + penalty * total
    basis = jnp.concatenate([hist_s, hist_y, gradient[None, :]], axis=0)
    narrow_basis = row_share(basis)
    gram_part = jnp.dot(
        narrow_basis, narrow_basis.T, precision=highest, preferred_element_type=jnp.float32
    )
    gram = lax.psum(gram_part, ("rows", "cols"))
    result = gram_recursion(gram, basis, newest)
    return (weights - step_length * result, gradient)


def solution(mesh):
    in_specs = (P("rows", "cols"), P("rows"), P("cols"), P(None, "cols"), P(None, "cols"), P())
    out_specs = (P("cols"), P("cols"))
    return jax.shard_map(body, mesh=mesh, in_specs=in_specs, out_specs=out_specs, check_vma=False)
```

profile of v0, /device:TPU:14, one launch (start us, length us, event | category | flops | bytes accessed | tf_op | source)
XLA Modules:
  0.0 156.8 jit_solution(8693725162735482173)
XLA Ops:
  0.6 0.8 convert_element_type.8
  1.4 5.6 %fusion.186 = f32[1,512]{1,0:T(1,128)S(1)} fusion(bf16[512,8192]{1,0:T(8,128)(2,1)} %param.6, bf16[8192,1]{0,1:T(2,128)(2,1)S(1)} %reshape.4), kind=kOutput, calls=%fused_computation.303 | convolution fusion | flops 8388608 | bytes 8407040 | tf_op jit(solution)/shard_map/dot_general | solution.py:48
  7.1 15.2 %psum.21 = f32[512]{0:T(512)S(1)} all-reduce(f32[512]{0:T(512)S(1)} %bitcast.507), channel_id=1, replica_groups=mesh['rows'=4,'cols'=8] {'cols'}, use_global_device_ids=true, to_apply=%region_0.0 | all-reduce | flops 512 | bytes 4096 | tf_op jit(solution)/shard_map/psum | solution.py:49
  22.3 4.7 %fusion.187 = f32[1,8192]{1,0:T(1,128)S(1)} fusion(bf16[512,1]{0,1:T(2,128)(2,1)S(1)} %reshape.6, bf16[512,8192]{1,0:T(8,128)(2,1)} %param.6), kind=kOutput, calls=%fused_computation.304 | convolution fusion | flops 8388608 | bytes 8422400 | tf_op jit(solution)/shard_map/dot_general | solution.py:51
  26.9 10.4 %psum.22 = f32[8192]{0:T(1024)S(1)} all-reduce(f32[8192]{0:T(1024)S(1)} %bitcast.505), channel_id=1, replica_groups=mesh['rows'=4,'cols'=8] {'rows'}, use_global_device_ids=true, to_apply=%region_1.2 | all-reduce | flops 8192 | bytes 65536 | tf_op jit(solution)/shard_map/psum | solution.py:53
  37.4 0.1 pad_maximum_fusion
  37.5 0.4 fusion.96
  37.9 45.6 %psum.23 = f32[33,33]{1,0:T(8,128)S(1)} all-reduce(f32[33,33]{1,0:T(8,128)S(1)} %fusion.96), channel_id=1, replica_groups=mesh['rows'=4,'cols'=8] {'rows','cols'}, use_global_device_ids=true, to_apply=%region_2.3 | all-reduce | flops 1089 | bytes 8712 | tf_op jit(solution)/shard_map/psum | solution.py:60
  84.2 0.7 fusion.48
  85.7 0.7 fusion.49
  87.1 0.7 fusion.50
  88.5 0.8 fusion.51
  90.0 0.7 fusion.52
  91.4 0.8 fusion.53
  92.8 0.7 fusion.56
  94.3 0.7 fusion.54
  95.7 0.8 fusion.55
  97.1 0.8 fusion.57
  98.6 0.7 fusion.60
  100.0 0.7 fusion.58
  101.5 0.8 fusion.59
  102.9 0.8 fusion.61
  104.3 0.7 fusion.64
  105.8 0.7 fusion.62
  107.2 0.8 fusion.63
  108.6 0.8 fusion.65
  110.1 0.7 fusion.68
  111.5 0.7 fusion.66
  113.0 0.8 fusion.67
  114.4 0.8 fusion.69
  115.8 0.7 fusion.72
  117.3 0.7 fusion.70
  118.7 0.8 fusion.71
  120.1 0.8 fusion.73
  121.6 0.7 fusion.76
  123.0 0.7 fusion.74
  124.5 0.8 fusion.75
  125.9 0.8 fusion.77
  127.3 0.7 fusion.78
  128.8 0.8 fusion.79
  130.2 0.8 fusion.121
  132.4 0.8 fusion.80
  133.8 0.8 fusion.81
  135.3 0.8 fusion.82
  136.7 0.8 fusion.83
  138.1 0.1 select_add_fusion.11
  138.2 0.8 fusion.84
  139.6 0.8 fusion.85
  141.0 0.1 select_add_fusion.9
  141.1 0.8 fusion.86
  142.5 0.8 fusion.87
  143.9 0.1 select_add_fusion.7
  144.0 0.8 fusion.88
  145.4 0.8 fusion.89
  146.8 0.1 select_add_fusion.5
  146.9 0.8 fusion.90
  148.3 0.8 fusion.91
  149.7 0.1 select_add_fusion.3
  149.8 0.8 fusion.92
  151.2 0.8 fusion.93
  152.6 0.8 fusion.94
  154.0 0.8 fusion.95
  155.4 0.7 fusion.124
  156.2 0.6 multiply_subtract_fusion
  (23 shorter events, 0.3 us)
Async XLA Ops:
  1.4 20.8 %copy-start.4 = (s32[512]{0:T(512)S(1)}, s32[512]{0:T(512)}, u32[]{:S(2)}) copy-start(s32[512]{0:T(512)} %param.7) | copy-start | bytes 6148
  22.2 15.1 %copy-start.2 = (f32[8192]{0:T(1024)S(1)}, f32[8192]{0:T(1024)}, u32[]{:S(2)}) copy-start(f32[8192]{0:T(1024)} %param.8) | copy-start | bytes 98308
  22.3 15.1 %copy-start = (f32[16,8192]{1,0:T(8,128)S(1)}, f32[16,8192]{1,0:T(8,128)}, u32[]{:S(2)}) copy-start(f32[16,8192]{1,0:T(8,128)} %param.10) | copy-start | bytes 1572868
  22.3 15.1 %copy-start.1 = (f32[16,8192]{1,0:T(8,128)S(1)}, f32[16,8192]{1,0:T(8,128)}, u32[]{:S(2)}) copy-start(f32[16,8192]{1,0:T(8,128)} %param.9) | copy-start | bytes 1572868
  37.4 118.1 %copy-start.3 = (f32[8192]{0:T(1024)}, f32[8192]{0:T(1024)S(1)}, u32[]{:S(2)}) copy-start(f32[8192]{0:T(1024)S(1)} %multiply_add_fusion) | copy-start | bytes 98308
where the time goes:
time: 158 us; the launch traced here: 157 us
  blocking collectives  71.2 us (45%)
  matrix products  48.3 us (31%)
  between operations  35.2 us (22%)
  other arithmetic  2.05 us (1%)
    psum x1, blocking collectives, body(): gram = lax.psum(gram_part, ('rows', 'cols'))  45.6 us
    dot_general x49, matrix products, quad_form(): jnp.dot(matrix, right, precision=highest)  36.8 us
    psum x1, blocking collectives, body(): margin = lax.psum(margin_part, 'cols')  15.2 us
    psum x1, blocking collectives, body(): total = lax.psum(total_part, 'rows')  10.4 us
    dot_general x1, matrix products, body(): jnp.dot(samples, weights.astype(jnp.bfloat16), preferred_element_type=jnp...  5.64 us
    dot_general x1, matrix products, body(): total_part = jnp.dot(resid, samples, preferred_element_type=jnp.float32)  4.66 us

commit v1 on v0

--- a/solution.py
+++ b/solution.py
@@ -1,3 +1,4 @@
+import functools
 import jax
 import jax.numpy as jnp
 from jax import lax
@@ -7,6 +8,19 @@
 penalty = 4.0
 step_length = 0.5
 highest = lax.Precision.HIGHEST
+
+
+def apply_bands_now(in_array, along_axis):
+    num = lax.axis_size(along_axis)
+    everything = lambda inter: [(j, j ^ inter) for j in range(num)]
+    prior = in_array
+    for dev_j in range(num.bit_length() - 1):
+        f_next = lax.ppermute(prior, along_axis, everything(1 << dev_j))
+        prior = prior + f_next
+    return prior
+
+
+make_column = functools.partial(apply_bands_now, along_axis="cols")
 
 
 def row_share(values):
@@ -46,7 +60,7 @@
 
 def body(samples, labels, weights, hist_s, hist_y, counter):
     margin_part = jnp.dot(samples, weights.astype(jnp.bfloat16), preferred_element_type=jnp.float32)
-    margin = lax.psum(margin_part, "cols")
+    margin = make_column(margin_part)
     resid = (jax.nn.sigmoid(margin) - labels.astype(jnp.float32)).astype(jnp.bfloat16)
     total_part = jnp.dot(resid, samples, preferred_element_type=jnp.float32)
     newest = counter[0] % HIST

time: 158 us -> 151 us (0.956)
  blocking collectives: 71.2 us -> 50.8 us
  waiting for transfers between devices: 0 us -> 7.24 us
  starting transfers between devices: 0 us -> 3.56 us
    psum x1 -> x0, blocking collectives: 15.2 us -> none  [body(): margin = lax.psum(margin_part, 'cols')]
    ppermute x0 -> x3, waiting for transfers between devices: none -> 7.24 us  [apply_bands_now(): f_next = lax.ppermute(prior, along_axis, everything(1 << dev_j))]
    psum x1, blocking collectives: 45.6 us -> 40.4 us  [body(): gram = lax.psum(gram_part, ('rows', 'cols'))]
    ppermute x0 -> x3, starting transfers between devices: none -> 3.56 us  [apply_bands_now(): f_next = lax.ppermute(prior, along_axis, everything(1 << dev_j))]
  transfers between devices with their start and end apart: 0 -> 3, of which waited for: 0 -> 3; matrix products, arithmetic and copies ran while one was open for 0% -> 0% of each run, Pallas kernels for 0% -> 0%
where the time goes in v1:
time: 151 us; the launch traced here: 149 us
  blocking collectives  50.8 us (34%)
  matrix products  49.5 us (33%)
  between operations  35.5 us (24%)
  waiting for transfers between devices  7.24 us (5%)
  starting transfers between devices  3.56 us (2%)
  other arithmetic  2.06 us (1%)
    psum x1, blocking collectives, body(): gram = lax.psum(gram_part, ('rows', 'cols'))  40.4 us
    dot_general x49, matrix products, quad_form(): jnp.dot(matrix, right, precision=highest)  38 us
    psum x1, blocking collectives, body(): total = lax.psum(total_part, 'rows')  10.4 us
    ppermute x3, waiting for transfers between devices, apply_bands_now(): f_next = lax.ppermute(prior, along_axis, everything(1 << dev_j))  7.24 us
    dot_general x1, matrix products, body(): jnp.dot(samples, weights.astype(jnp.bfloat16), preferred_element_type=jnp...  5.64 us
    dot_general x1, matrix products, body(): total_part = jnp.dot(resid, samples, preferred_element_type=jnp.float32)  4.66 us
    ppermute x3, starting transfers between devices, apply_bands_now(): f_next = lax.ppermute(prior, along_axis, everything(1 << dev_j))  3.56 us
  transfers between devices with their start and end apart: 3, of which 3 were waited for; matrix products, arithmetic and copies ran while one was open for 0% of the time, Pallas kernels for 0%

profile of v1, /device:TPU:14, one launch (start us, length us, event | category | flops | bytes accessed | tf_op | source)
XLA Modules:
  0.0 148.7 jit_solution(17330167757967100074)
XLA Ops:
  0.6 0.8 convert_element_type.8
  1.4 5.6 %fusion.186 = f32[1,512]{1,0:T(1,128)S(1)} fusion(bf16[512,8192]{1,0:T(8,128)(2,1)} %param.6, bf16[8192,1]{0,1:T(2,128)(2,1)S(1)} %reshape.4), kind=kOutput, calls=%fused_computation.303 | convolution fusion | flops 8388608 | bytes 8407040 | tf_op jit(solution)/shard_map/dot_general | solution.py:62
  7.1 0.5 collective-permute-start
  8.5 2.2 %collective-permute-done = f32[512]{0:T(512)S(1)} collective-permute-done((f32[512]{0:T(512)S(1)}, f32[512]{0:T(512)S(1)}, u32[]{:S(2)}, u32[]{:S(2)}) %collective-permute-start) | collective-permute-done | bytes 2080 | tf_op jit(solution)/shard_map/ppermute | solution.py:18
  10.7 0.4 collective-permute-start.1
  11.1 3.1 %collective-permute-done.1 = f32[512]{0:T(512)S(1)} collective-permute-done((f32[512]{0:T(512)S(1)}, f32[512]{0:T(512)S(1)}, u32[]{:S(2)}, u32[]{:S(2)}) %collective-permute-start.1) | collective-permute-done | bytes 2080 | tf_op jit(solution)/shard_map/ppermute | solution.py:18
  14.3 2.6 %collective-permute-start.2 = (f32[512]{0:T(512)S(1)}, f32[512]{0:T(512)S(1)}, u32[]{:S(2)}, u32[]{:S(2)}) collective-permute-start(f32[512]{0:T(512)S(1)} %add.190), channel_id=1, source_target_pairs={{0,4},{1,5},{2,6},{3,7},{4,0},{5,1},{6,2},{7,3},{8,12},{9,13},{10,... | collective-permute-start | bytes 6152 | tf_op jit(solution)/shard_map/ppermute | solution.py:18
  16.9 1.9 %collective-permute-done.2 = f32[512]{0:T(512)S(1)} collective-permute-done((f32[512]{0:T(512)S(1)}, f32[512]{0:T(512)S(1)}, u32[]{:S(2)}, u32[]{:S(2)}) %collective-permute-start.2) | collective-permute-done | bytes 2080 | tf_op jit(solution)/shard_map/ppermute | solution.py:18
  18.8 4.7 %fusion.187 = f32[1,8192]{1,0:T(1,128)S(1)} fusion(bf16[512,1]{0,1:T(2,128)(2,1)S(1)} %reshape.6, bf16[512,8192]{1,0:T(8,128)(2,1)} %param.6), kind=kOutput, calls=%fused_computation.304 | convolution fusion | flops 8388608 | bytes 8422400 | tf_op jit(solution)/shard_map/dot_general | solution.py:65
  23.5 10.4 %psum.14 = f32[8192]{0:T(1024)S(1)} all-reduce(f32[8192]{0:T(1024)S(1)} %bitcast.505), channel_id=1, replica_groups=mesh['rows'=4,'cols'=8] {'rows'}, use_global_device_ids=true, to_apply=%region_0.1 | all-reduce | flops 8192 | bytes 65536 | tf_op jit(solution)/shard_map/psum | solution.py:67
  33.9 0.1 pad_maximum_fusion
  34.0 0.4 fusion.96
  34.5 40.4 %psum.15 = f32[33,33]{1,0:T(8,128)S(1)} all-reduce(f32[33,33]{1,0:T(8,128)S(1)} %fusion.96), channel_id=1, replica_groups=mesh['rows'=4,'cols'=8] {'rows','cols'}, use_global_device_ids=true, to_apply=%region_1.2 | all-reduce | flops 1089 | bytes 8712 | tf_op jit(solution)/shard_map/psum | solution.py:74
  74.9 0.8 fusion.49
  75.7 0.7 fusion.48
  76.5 0.7 fusion.50
  79.2 0.8 fusion.51
  79.9 0.8 fusion.52
  82.1 0.8 fusion.53
  82.9 0.8 fusion.56
  84.5 0.8 fusion.54
  86.7 0.8 fusion.55
  88.1 0.8 fusion.57
  88.8 0.8 fusion.60
  90.4 0.8 fusion.58
  92.6 0.8 fusion.59
  94.0 0.8 fusion.61
  94.8 0.8 fusion.64
  96.3 0.8 fusion.62
  98.6 0.8 fusion.63
  100.0 0.8 fusion.65
  100.7 0.8 fusion.68
  102.3 0.8 fusion.66
  104.5 0.8 fusion.67
  105.9 0.8 fusion.69
  106.7 0.8 fusion.72
  108.2 0.8 fusion.70
  110.5 0.8 fusion.71
  111.9 0.8 fusion.73
  112.6 0.8 fusion.76
  114.2 0.8 fusion.74
  116.4 0.8 fusion.75
  117.8 0.8 fusion.77
  118.6 0.8 fusion.78
  120.8 0.8 fusion.79
  121.6 0.8 fusion.121
  124.4 0.8 fusion.80
  125.8 0.8 fusion.81
  127.3 0.8 fusion.82
  128.7 0.8 fusion.83
  130.1 0.8 fusion.84
  131.6 0.8 fusion.85
  133.0 0.8 fusion.86
  134.4 0.8 fusion.87
  135.9 0.8 fusion.88
  137.3 0.8 fusion.89
  138.8 0.8 fusion.90
  140.2 0.8 fusion.91
  141.7 0.8 fusion.92
  143.1 0.8 fusion.93
  144.5 0.8 fusion.94
  146.0 0.8 fusion.95
  147.4 0.7 fusion.124
  148.1 0.6 multiply_subtract_fusion
  (30 shorter events, 0.6 us)
Async XLA Ops:
  1.4 17.3 %copy-start.4 = (s32[512]{0:T(512)S(1)}, s32[512]{0:T(512)}, u32[]{:S(2)}) copy-start(s32[512]{0:T(512)} %param.7) | copy-start | bytes 6148
  7.1 3.6 %collective-permute-start = (f32[512]{0:T(512)S(1)}, f32[512]{0:T(512)S(1)}, u32[]{:S(2)}, u32[]{:S(2)}) collective-permute-start(f32[512]{0:T(512)S(1)} %bitcast.507), channel_id=1, source_target_pairs={{0,1},{1,0},{2,3},{3,2},{4,5},{5,4},{6,7},{7,6},{8,9},{9,8},{10,11... | collective-permute-start | bytes 6152 | tf_op jit(solution)/shard_map/ppermute | solution.py:18
  10.7 3.6 %collective-permute-start.1 = (f32[512]{0:T(512)S(1)}, f32[512]{0:T(512)S(1)}, u32[]{:S(2)}, u32[]{:S(2)}) collective-permute-start(f32[512]{0:T(512)S(1)} %add.189), channel_id=1, source_target_pairs={{0,2},{1,3},{2,0},{3,1},{4,6},{5,7},{6,4},{7,5},{8,10},{9,11},{10,... | collective-permute-start | bytes 6152 | tf_op jit(solution)/shard_map/ppermute | solution.py:18
  14.3 4.5 %collective-permute-start.2 = (f32[512]{0:T(512)S(1)}, f32[512]{0:T(512)S(1)}, u32[]{:S(2)}, u32[]{:S(2)}) collective-permute-start(f32[512]{0:T(512)S(1)} %add.190), channel_id=1, source_target_pairs={{0,4},{1,5},{2,6},{3,7},{4,0},{5,1},{6,2},{7,3},{8,12},{9,13},{10,... | collective-permute-start | bytes 6152 | tf_op jit(solution)/shard_map/ppermute | solution.py:18
  18.8 15.1 %copy-start.2 = (f32[8192]{0:T(1024)S(1)}, f32[8192]{0:T(1024)}, u32[]{:S(2)}) copy-start(f32[8192]{0:T(1024)} %param.8) | copy-start | bytes 98308
  18.8 15.1 %copy-start = (f32[16,8192]{1,0:T(8,128)S(1)}, f32[16,8192]{1,0:T(8,128)}, u32[]{:S(2)}) copy-start(f32[16,8192]{1,0:T(8,128)} %param.10) | copy-start | bytes 1572868
  18.8 15.1 %copy-start.1 = (f32[16,8192]{1,0:T(8,128)S(1)}, f32[16,8192]{1,0:T(8,128)}, u32[]{:S(2)}) copy-start(f32[16,8192]{1,0:T(8,128)} %param.9) | copy-start | bytes 1572868
  33.9 113.5 %copy-start.3 = (f32[8192]{0:T(1024)}, f32[8192]{0:T(1024)S(1)}, u32[]{:S(2)}) copy-start(f32[8192]{0:T(1024)S(1)} %multiply_add_fusion) | copy-start | bytes 98308

commit v2 on v0

--- a/solution.py
+++ b/solution.py
@@ -7,6 +7,7 @@
 penalty = 4.0
 step_length = 0.5
 highest = lax.Precision.HIGHEST
+fit_regions = lambda vector, lane_axis, bus_axis: lax.psum(lax.psum(vector, lane_axis), bus_axis)
 
 
 def row_share(values):
@@ -57,7 +58,7 @@
     gram_part = jnp.dot(
         narrow_basis, narrow_basis.T, precision=highest, preferred_element_type=jnp.float32
     )
-    gram = lax.psum(gram_part, ("rows", "cols"))
+    gram = fit_regions(gram_part, "cols", "rows")
     result = gram_recursion(gram, basis, newest)
     return (weights - step_length * result, gradient)
 

time: 158 us -> 163 us (1.032)
  the two profiles are of different devices: /device:TPU:14 before, /device:TPU:0 now
where the time goes in v2:
time: 163 us; the launch traced here: 162 us
  blocking collectives  76.7 us (47%)
  matrix products  48.3 us (30%)
  between operations  35.2 us (22%)
  other arithmetic  2.05 us (1%)
    dot_general x49, matrix products, quad_form(): jnp.dot(matrix, right, precision=highest)  36.8 us
    psum x1, blocking collectives, lax.psum(vector, lane_axis)  33 us
    psum x1, blocking collectives, body(): margin = lax.psum(margin_part, 'cols')  23.1 us
    psum x1, blocking collectives, body(): total = lax.psum(total_part, 'rows')  10.3 us
    psum x1, blocking collectives, lax.psum(lax.psum(vector, lane_axis), bus_axis)  10.2 us
    dot_general x1, matrix products, body(): jnp.dot(samples, weights.astype(jnp.bfloat16), preferred_element_type=jnp...  5.64 us
    dot_general x1, matrix products, body(): total_part = jnp.dot(resid, samples, preferred_element_type=jnp.float32)  4.66 us

profile of v2, /device:TPU:0, one launch (start us, length us, event | category | flops | bytes accessed | tf_op | source)
XLA Modules:
  0.0 162.3 jit_solution(14291415026281240174)
XLA Ops:
  0.6 0.8 convert_element_type.8
  1.4 5.6 %fusion.186 = f32[1,512]{1,0:T(1,128)S(1)} fusion(bf16[512,8192]{1,0:T(8,128)(2,1)} %param.6, bf16[8192,1]{0,1:T(2,128)(2,1)S(1)} %reshape.4), kind=kOutput, calls=%fused_computation.303 | convolution fusion | flops 8388608 | bytes 8407040 | tf_op jit(solution)/shard_map/dot_general | solution.py:49
  7.1 23.1 %psum.28 = f32[512]{0:T(512)S(1)} all-reduce(f32[512]{0:T(512)S(1)} %bitcast.507), channel_id=1, replica_groups=mesh['rows'=4,'cols'=8] {'cols'}, use_global_device_ids=true, to_apply=%region_0.0 | all-reduce | flops 512 | bytes 4096 | tf_op jit(solution)/shard_map/psum | solution.py:50
  30.3 4.7 %fusion.187 = f32[1,8192]{1,0:T(1,128)S(1)} fusion(bf16[512,1]{0,1:T(2,128)(2,1)S(1)} %reshape.6, bf16[512,8192]{1,0:T(8,128)(2,1)} %param.6), kind=kOutput, calls=%fused_computation.304 | convolution fusion | flops 8388608 | bytes 8422400 | tf_op jit(solution)/shard_map/dot_general | solution.py:52
  34.9 10.3 %psum.29 = f32[8192]{0:T(1024)S(1)} all-reduce(f32[8192]{0:T(1024)S(1)} %bitcast.505), channel_id=1, replica_groups=mesh['rows'=4,'cols'=8] {'rows'}, use_global_device_ids=true, to_apply=%region_1.2 | all-reduce | flops 8192 | bytes 65536 | tf_op jit(solution)/shard_map/psum | solution.py:54
  45.3 0.1 pad_maximum_fusion
  45.4 0.4 fusion.96
  45.8 33.0 %psum.30 = f32[33,33]{1,0:T(8,128)S(1)} all-reduce(f32[33,33]{1,0:T(8,128)S(1)} %fusion.96), channel_id=1, replica_groups=mesh['rows'=4,'cols'=8] {'cols'}, use_global_device_ids=true, to_apply=%region_2.3 | all-reduce | flops 1089 | bytes 8712 | tf_op jit(solution)/shard_map/psum | solution.py:10
  78.8 10.2 %psum.31 = f32[33,33]{1,0:T(8,128)S(1)} all-reduce(f32[33,33]{1,0:T(8,128)S(1)} %psum.30), channel_id=1, replica_groups=mesh['rows'=4,'cols'=8] {'rows'}, use_global_device_ids=true, to_apply=%region_3.4 | all-reduce | flops 1089 | bytes 8712 | tf_op jit(solution)/shard_map/psum | solution.py:10
  89.7 0.7 fusion.48
  91.2 0.7 fusion.49
  92.6 0.7 fusion.50
  94.0 0.8 fusion.51
  95.5 0.7 fusion.52
  96.9 0.8 fusion.53
  98.3 0.7 fusion.56
  99.8 0.7 fusion.54
  101.2 0.8 fusion.55
  102.6 0.8 fusion.57
  104.1 0.7 fusion.60
  105.5 0.7 fusion.58
  107.0 0.8 fusion.59
  108.4 0.8 fusion.61
  109.8 0.7 fusion.64
  111.3 0.7 fusion.62
  112.7 0.8 fusion.63
  114.1 0.8 fusion.65
  115.6 0.7 fusion.68
  117.0 0.7 fusion.66
  118.5 0.8 fusion.67
  119.9 0.8 fusion.69
  121.3 0.7 fusion.72
  122.8 0.7 fusion.70
  124.2 0.8 fusion.71
  125.6 0.8 fusion.73
  127.1 0.7 fusion.76
  128.5 0.7 fusion.74
  130.0 0.8 fusion.75
  131.4 0.8 fusion.77
  132.8 0.7 fusion.78
  134.3 0.8 fusion.79
  135.7 0.8 fusion.121
  137.9 0.8 fusion.80
  139.3 0.8 fusion.81
  140.8 0.8 fusion.82
  142.2 0.8 fusion.83
  143.7 0.8 fusion.84
  145.1 0.8 fusion.85
  146.5 0.1 select_add_fusion.9
  146.6 0.8 fusion.86
  148.0 0.8 fusion.87
  149.4 0.1 select_add_fusion.7
  149.5 0.8 fusion.88
  150.9 0.8 fusion.89
  152.3 0.1 select_add_fusion.5
  152.4 0.8 fusion.90
  153.8 0.8 fusion.91
  155.2 0.1 select_add_fusion.3
  155.3 0.8 fusion.92
  156.7 0.8 fusion.93
  158.1 0.8 fusion.94
  159.5 0.8 fusion.95
  160.9 0.7 fusion.124
  161.7 0.6 multiply_subtract_fusion
  (24 shorter events, 0.4 us)
Async XLA Ops:
  1.4 28.8 %copy-start.4 = (s32[512]{0:T(512)S(1)}, s32[512]{0:T(512)}, u32[]{:S(2)}) copy-start(s32[512]{0:T(512)} %param.7) | copy-start | bytes 6148
  30.2 15.0 %copy-start.2 = (f32[8192]{0:T(1024)S(1)}, f32[8192]{0:T(1024)}, u32[]{:S(2)}) copy-start(f32[8192]{0:T(1024)} %param.8) | copy-start | bytes 98308
  30.3 15.0 %copy-start = (f32[16,8192]{1,0:T(8,128)S(1)}, f32[16,8192]{1,0:T(8,128)}, u32[]{:S(2)}) copy-start(f32[16,8192]{1,0:T(8,128)} %param.10) | copy-start | bytes 1572868
  30.3 15.0 %copy-start.1 = (f32[16,8192]{1,0:T(8,128)S(1)}, f32[16,8192]{1,0:T(8,128)}, u32[]{:S(2)}) copy-start(f32[16,8192]{1,0:T(8,128)} %param.9) | copy-start | bytes 1572868
  45.2 115.7 %copy-start.3 = (f32[8192]{0:T(1024)}, f32[8192]{0:T(1024)S(1)}, u32[]{:S(2)}) copy-start(f32[8192]{0:T(1024)S(1)} %multiply_add_fusion) | copy-start | bytes 98308
